TPU v7x, 32 devices: a whole 2x2x4 slice. The times are simulated.
32 devices in a mesh: paths: 4 (over x, core), cpty: 8 (over z, y).
Axes of the slice: x: 2, y: 2, z: 4, core: 2. Of those that a mesh axis runs over, the one named last changes fastest.
Arguments:
- factors: bfloat16 [64, 6144], P(None, 'paths'), may hold values from -6 to 6
- loadings: bfloat16 [64, 16384], P(None, 'cpty'), may hold values from -2 to 2
- notional: bfloat16 [16384], P('cpty'), may hold values from 0.25 to 0.796875
- strike: bfloat16 [16384], P('cpty'), may hold values from 2 to 8
- curvature: bfloat16 [16384], P('cpty'), may hold values from 1 to 3
- trade_cpty: int32 [16384], P('cpty'), may hold values from 0 to 1023, as said below
Outputs:
- exposure: bfloat16 [6144, 1024], P('paths', 'cpty')
- moment: float32 [1024, 1024], P('paths', 'cpty')
Inputs may be any that keep to these rules, and one draw needn't show every extreme that they name: `trade_cpty`: of the trades in the book of one index of cpty, at most 512 belong to the counterparties numbered k * 128 to (k + 1) * 128 - 1 for any k; in every draw some such k receives exactly 512 from every book.
All inputs are finite; a program needn't handle non-finite values.
Results may differ from a plain program's by a relative error of at most 0.0064.
Values may be sent and summed in bfloat16 or wider, within the bound.
No kernel may reach another device: no remote copies, remote signals or barrier semaphores. Data moves between devices by JAX's collectives and lax.ppermute only.
A program may use at most 128 MiB of HBM per device.

v0:
```python
import jax
import jax.numpy as jnp
from jax import lax
from jax.sharding import PartitionSpec as P

CP_DEV = 128


def price_trades(drivers, loading_cols, trade_terms):
    linear = jnp.dot(drivers, loading_cols, preferred_element_type=jnp.float32)
    terms_wide = trade_terms.astype(jnp.float32)
    value = terms_wide[0] * (linear + terms_wide[2] * jnp.tanh(linear - terms_wide[1]))
    return value.astype(jnp.bfloat16)


def on_device(factors, loadings, notional, strike, curvature, trade_cpty):
    groups = lax.axis_size("cpty")
    own_index = lax.axis_index("cpty")
    trades = loadings.shape[1]
    slot_size = 2 * trades // groups
    owners = trade_cpty // CP_DEV
    marked = (owners[:, None] == jnp.arange(groups, dtype=jnp.int32)[None, :]).astype(jnp.int32)
    ranking = jnp.sum((jnp.cumsum(marked, axis=0) - marked) * marked, axis=1)
    target = owners * slot_size + ranking
    chosen = (
        jnp.zeros((groups * slot_size,), jnp.int32)
        .at[target]
        .set(jnp.arange(trades, dtype=jnp.int32))
    )
    filled = jnp.zeros((groups * slot_size,), jnp.bool_).at[target].set(True)
    labels = jnp.where(filled, trade_cpty[chosen], -1)[None, :]
    drivers = jnp.transpose(factors)
    trade_terms = jnp.stack([notional, strike, curvature])
    described = jnp.concatenate([loadings, trade_terms], axis=0)
    packed = jnp.where(
        filled[None, :], jnp.take(described, chosen, axis=1), jnp.zeros((), jnp.bfloat16)
    )
    received, arrived_ids = (
        lax.all_to_all(packed, "cpty", split_axis=1, concat_axis=1, tiled=True),
        lax.all_to_all(labels, "cpty", split_axis=1, concat_axis=1, tiled=True),
    )
    factor_count = loadings.shape[0]
    arrived = price_trades(drivers, received[:factor_count], received[factor_count:])
    local_ids = arrived_ids[0] - own_index * CP_DEV
    onehot = (local_ids[:, None] == jnp.arange(CP_DEV, dtype=jnp.int32)[None, :]).astype(
        jnp.bfloat16
    )
    netted = jnp.dot(arrived, onehot, preferred_element_type=jnp.float32)
    exposure = jnp.maximum(netted, 0.0).astype(jnp.bfloat16)
    everyone = lax.all_gather(exposure, "cpty", axis=1, tiled=True)
    path_total = exposure.shape[0] * lax.axis_size("paths")
    moment = (
        lax.psum_scatter(
            jnp.einsum("pa,pb->ab", everyone, exposure, preferred_element_type=jnp.float32),
            "paths",
            scatter_dimension=0,
            tiled=True,
        )
        / path_total
    )
    return (exposure, moment)


def solution(mesh):
    in_specs = (P(None, "paths"), P(None, "cpty"), P("cpty"), P("cpty"), P("cpty"), P("cpty"))
    out_specs = (P("paths", "cpty"), P("paths", "cpty"))
    return jax.shard_map(
        on_device, mesh=mesh, in_specs=in_specs, out_specs=out_specs, check_vma=False
    )
```

profile of v0, /device:TPU:0, one launch (start us, length us, event | category | flops | bytes accessed | tf_op | source)
XLA Modules:
  0.0 204.9 jit_solution(14715116246756037690)
XLA Ops:
  7.2 0.0 copy-start
  7.2 0.8 add_select_fusion
  8.0 2.3 %reduce-window.6 = s32[8,16,128]{2,1,0:T(8,128)S(1)} reduce-window(s32[8,16,128]{2,1,0:T(8,128)S(1)} %fusion.14, s32[]{:T(128)} %constant.24.clone.1), window={size=1x1x128 pad=0_0x0_0x127_0}, to_apply=%region_0.1 | reduce-window | flops 2080768 | bytes 131076 | tf_op jit(solution)/shard_map/reduce-window
  10.3 0.3 slice_reduce_fusion
  10.5 0.2 reduce-window.9
  10.7 0.1 add_bitcast_fusion
  10.9 0.7 compare_select_fusion.1
  11.6 8.1 %scatter_custom_fusion.1 = s32[4096]{0:T(1024)S(1)} fusion(s32[2048]{0:T(1024)S(1)} %compare_select_fusion.1, s32[2048]{0:T(1024)S(1)} %iota.15, s32[]{:T(128)} %constant.24.clone.1), kind=kCustom, calls=%fused_computation.43 | custom fusion | bytes 16388 | tf_op jit(solution)/shard_map/scatter | solution.py:28
  19.7 23.0 %gather_fusion.1 = s32[4096]{0:T(1024)S(1)} fusion(s32[2048]{0:T(1024)S(1)} %copy-done.1, s32[4096]{0:T(1024)S(1)} %fusion.15), kind=kCustom, calls=%fused_computation.1 | custom fusion | bytes 49152 | tf_op jit(solution)/shard_map/gather | solution.py:31
  42.8 9.1 %scatter_custom_fusion = pred[4096]{0:T(1024)(128)(4,1)S(1)} fusion(s32[2048]{0:T(1024)S(1)} %compare_select_fusion.1, pred[2048]{0:T(1024)(128)(4,1)S(1)} %broadcast.49, pred[]{:T(512)} %constant.22.clone.1), kind=kCustom, calls=%fused_computation.47 | custom fusion | bytes 4097 | tf_op jit(solution)/shard_map/scatter | solution.py:30
  51.9 0.6 broadcast_select_fusion
  52.5 7.3 %all-to-all-start.1 = ((s32[1,8,512]{2,0,1:T(1,128)}), s32[1,8,512]{2,0,1:T(1,128)S(1)}, u32[]{:S(2)}, u32[]{:S(2)}) async-start(s32[1,8,512]{2,0,1:T(1,128)} %bitcast.8), calls=%async_computation.1 | async-start | bytes 32768 | tf_op jit(solution)/shard_map/all_to_all | solution.py:40
  59.9 0.3 copy.19
  60.2 0.3 stack.12
  60.5 0.3 stack.13
  60.9 0.3 stack.14
  61.2 0.7 pad_maximum_fusion
  61.9 12.1 %gather_fusion = bf16[4096,67]{1,0:T(8,128)(2,1)S(1)} fusion(bf16[67,2048]{0,1:T(8,128)(2,1)S(1)} %pad_maximum_fusion, s32[4096]{0:T(1024)S(1)} %fusion.15), kind=kCustom, calls=%fused_computation | custom fusion | bytes 1114112 | tf_op jit(solution)/shard_map/jit(_take)/gather | solution.py:36
  74.1 0.6 copy.23
  74.6 0.9 select_select_fusion
  75.5 6.0 %all-to-all-start = ((bf16[67,8,512]{2,0,1:T(8,128)(2,1)}), bf16[67,8,512]{2,0,1:T(8,128)(2,1)S(1)}, u32[]{:S(2)}, u32[]{:S(2)}) async-start(bf16[67,8,512]{2,0,1:T(8,128)(2,1)} %select_select_fusion), calls=%async_computation | async-start | bytes 1179648 | tf_op jit(solution)/shard_map/all_to_all | solution.py:39
  81.5 0.0 all-gather.2.cloned.1.call-start
  81.6 0.9 iota_compare_fusion.7
  82.5 14.4 %all-to-all-done = bf16[67,8,512]{2,0,1:T(8,128)(2,1)S(1)} async-done(((bf16[67,8,512]{2,0,1:T(8,128)(2,1)}), bf16[67,8,512]{2,0,1:T(8,128)(2,1)S(1)}, u32[]{:S(2)}, u32[]{:S(2)}) %all-to-all-start) | async-done | bytes 548896 | tf_op jit(solution)/shard_map/all_to_all | solution.py:39
  97.1 13.8 %fusion.9 = bf16[1536,128]{1,0:T(8,128)(2,1)} fusion(bf16[64,4096]{1,0:T(8,128)(2,1)S(1)} %bitcast.70, bf16[64,1536]{1,0:T(8,128)(2,1)S(1)} %copy-done, f32[4096]{0:T(1024)S(1)} %bitcast.75, f32[4096]{0:T(1024)S(1)} %bitcast.76, f32[4096]{0:T(1024)S(1)} %bitcast.74, pred[4096,128]{1,0:T(32,128)(4,1)S(1)} %iota_compare_fusion.7), kind=kOutput, calls=%fused_computation.15 | convolution fusion | flops 2447769600 | bytes 1687552 | tf_op jit(solution)/shard_map/dot_general | solution.py:48
  110.8 0.0 all-gather.2.cloned.1.call-update
  110.9 0.0 reduce-scatter.2.cloned.1.call-start
  110.9 61.8 %all-gather.2.cloned.1.call-done = bf16[1536,1024]{1,0:T(8,128)(2,1)} async-done(((bf16[1536,128]{1,0:T(8,128)(2,1)}), bf16[1536,1024]{1,0:T(8,128)(2,1)}) %all-gather.2.cloned.1.call-update) | async-done | bytes 3145744 | tf_op jit(solution)/shard_map/all_gather | solution.py:50
  172.7 3.7 %fusion.24 = f32[1024,128]{1,0:T(8,128)} fusion(bf16[1536,1024]{1,0:T(8,128)(2,1)} %all-gather.2.cloned.1.call-done, bf16[1536,128]{1,0:T(8,128)(2,1)} %fusion.9), kind=kOutput, calls=%fused_computation.51 | convolution fusion | flops 402653184 | bytes 4063232 | tf_op jit(solution)/shard_map/pa,pb->ab/dot_general | solution.py:54
  176.5 0.0 reduce-scatter.2.cloned.1.call-update
  176.5 20.0 %reduce-scatter.2.cloned.1.call-done = f32[256,128]{1,0:T(8,128)} async-done(((f32[1024,128]{1,0:T(8,128)}), f32[256,128]{1,0:T(8,128)}) %reduce-scatter.2.cloned.1.call-update) | async-done | bytes 131088 | tf_op jit(solution)/shard_map/reduce_scatter | solution.py:53
  196.4 1.6 broadcast_multiply_fusion
  (25 shorter events, 0.3 us)
Async XLA Ops:
  7.2 89.9 %copy-start = (bf16[64,1536]{1,0:T(8,128)(2,1)S(1)}, bf16[64,1536]{1,0:T(8,128)(2,1)}, u32[]{:S(2)}) copy-start(bf16[64,1536]{1,0:T(8,128)(2,1)} %param.6) | copy-start | bytes 589828
  7.2 12.5 %copy-start.1 = (s32[2048]{0:T(1024)S(1)}, s32[2048]{0:T(1024)}, u32[]{:S(2)}) copy-start(s32[2048]{0:T(1024)} %param.11) | copy-start | bytes 24580
  19.7 40.2 %copy-start.2 = (bf16[64,2048]{1,0:T(8,128)(2,1)S(1)}, bf16[64,2048]{1,0:T(8,128)(2,1)}, u32[]{:S(2)}) copy-start(bf16[64,2048]{1,0:T(8,128)(2,1)} %param.7) | copy-start | bytes 786436
  19.7 40.5 %copy-start.3 = (bf16[2048]{0:T(1024)(128)(2,1)S(1)}, bf16[2048]{0:T(1024)(128)(2,1)}, u32[]{:S(2)}) copy-start(bf16[2048]{0:T(1024)(128)(2,1)} %param.8) | copy-start | bytes 12292
  19.7 40.8 %copy-start.4 = (bf16[2048]{0:T(1024)(128)(2,1)S(1)}, bf16[2048]{0:T(1024)(128)(2,1)}, u32[]{:S(2)}) copy-start(bf16[2048]{0:T(1024)(128)(2,1)} %param.9) | copy-start | bytes 12292
  19.7 41.2 %copy-start.5 = (bf16[2048]{0:T(1024)(128)(2,1)S(1)}, bf16[2048]{0:T(1024)(128)(2,1)}, u32[]{:S(2)}) copy-start(bf16[2048]{0:T(1024)(128)(2,1)} %param.10) | copy-start | bytes 12292
  52.5 23.0 %all-to-all-start.1 = ((s32[1,8,512]{2,0,1:T(1,128)}), s32[1,8,512]{2,0,1:T(1,128)S(1)}, u32[]{:S(2)}, u32[]{:S(2)}) async-start(s32[1,8,512]{2,0,1:T(1,128)} %bitcast.8), calls=%async_computation.1 | async-start | bytes 32768 | tf_op jit(solution)/shard_map/all_to_all | solution.py:40
  75.5 21.4 %all-to-all-start = ((bf16[67,8,512]{2,0,1:T(8,128)(2,1)}), bf16[67,8,512]{2,0,1:T(8,128)(2,1)S(1)}, u32[]{:S(2)}, u32[]{:S(2)}) async-start(bf16[67,8,512]{2,0,1:T(8,128)(2,1)} %select_select_fusion), calls=%async_computation | async-start | bytes 1179648 | tf_op jit(solution)/shard_map/all_to_all | solution.py:39
  81.5 91.2 %all-gather.2.cloned.1.call-start = ((), (), s32[]{:S(2)}) async-start(), calls=%async_computation.3 | async-start | bytes 3538944 | tf_op jit(solution)/shard_map/all_gather | solution.py:50
  110.9 85.6 %reduce-scatter.2.cloned.1.call-start = ((), (), s32[]{:S(2)}) async-start(), calls=%async_computation.4 | async-start | bytes 655360 | tf_op jit(solution)/shard_map/reduce_scatter | solution.py:53
Sparse Core Ops, SparseCore 0:
  111.0 61.6 all-gather.1
  176.6 19.7 reduce-scatter.1
where the time goes:
time: 205 us
  waiting for transfers between devices  96.2 us (47%)
  local copies, waits for them, and re-layouts  54.7 us (27%)
  matrix products  17.5 us (9%)
  between operations  14.3 us (7%)
  starting transfers between devices  13.4 us (7%)
  other arithmetic  8.76 us (4%)
    all_gather x1, waiting for transfers between devices, on_device(): everyone = lax.all_gather(exposure, 'cpty', axis=1, tiled=True)  61.8 us
    gather x1, local copies, waits for them, and re-layouts, on_device(): labels = jnp.where(filled, trade_cpty[chosen], -1)[None, :]  23 us
    reduce_scatter x1, waiting for transfers between devices, on_device(): lax.psum_scatter(jnp.einsum('pa,pb->ab', everyone, exposure, preferred_el...  20 us
    all_to_all x1, waiting for transfers between devices, on_device(): lax.all_to_all(packed, 'cpty', split_axis=1, concat_axis=1, tiled=True)  14.4 us
    dot_general x1, matrix products, on_device(): netted = jnp.dot(arrived, onehot, preferred_element_type=jnp.float32)  13.8 us
    gather x2, local copies, waits for them, and re-layouts, on_device(): jnp.take(described, chosen, axis=1)  12.7 us
    scatter x1, local copies, waits for them, and re-layouts, on_device(): filled = jnp.zeros((groups * slot_size,), jnp.bool_).at[target].set(True)  9.13 us
    scatter x1, local copies, waits for them, and re-layouts, on_device(): chosen = jnp.zeros((groups * slot_size,), jnp.int32).at[target].set(jnp.a...  8.06 us
  transfers between devices with their start and end apart: 4, of which 3 were waited for; matrix products, arithmetic and copies ran while one was open for 8% of the time, Pallas kernels for 0%

commit v1 on v0

--- a/solution.py
+++ b/solution.py
@@ -4,6 +4,31 @@
 from jax.sharding import PartitionSpec as P
 
 CP_DEV = 128
+
+
+def laid_out(blocks, dim):
+    dims = list(blocks.shape[1:])
+    dims[dim] *= blocks.shape[0]
+    return jnp.moveaxis(blocks, 0, dim).reshape(dims)
+
+
+def on_each_block(x, axis, dim, apply, out_dim):
+    size, index, span = (lax.axis_size(axis), lax.axis_index(axis), x.shape[dim])
+    forward = [(i, (i + 1) % size) for i in range(size)]
+    left = [(i, (i - 1) % size) for i in range(size)]
+    half = size // 2
+    parts = {}
+    from_left = from_right = x
+    for step in range(half + 1):
+        next_left = lax.ppermute(from_left, axis, forward) if step < half else None
+        next_right = lax.ppermute(from_right, axis, left) if step < size - half - 1 else None
+        parts[-step] = apply(from_left, (index - step) % size * span)
+        if 0 < step < size - half:
+            parts[step] = apply(from_right, (index + step) % size * span)
+        from_left, from_right = (next_left, next_right)
+    parts = jnp.stack([parts[k] for k in sorted(parts)])
+    parts = parts[(jnp.arange(size) - index + half) % size]
+    return laid_out(parts, out_dim)
 
 
 def price_trades(drivers, loading_cols, trade_terms):
@@ -47,11 +72,18 @@
     )
     netted = jnp.dot(arrived, onehot, preferred_element_type=jnp.float32)
     exposure = jnp.maximum(netted, 0.0).astype(jnp.bfloat16)
-    everyone = lax.all_gather(exposure, "cpty", axis=1, tiled=True)
     path_total = exposure.shape[0] * lax.axis_size("paths")
     moment = (
         lax.psum_scatter(
-            jnp.einsum("pa,pb->ab", everyone, exposure, preferred_element_type=jnp.float32),
+            on_each_block(
+                exposure,
+                "cpty",
+                1,
+                lambda shard, offset: jnp.einsum(
+                    "pa,pb->ab", shard, exposure, preferred_element_type=jnp.float32
+                ),
+                0,
+            ),
             "paths",
             scatter_dimension=0,
             tiled=True,

time: 205 us -> 207 us (level)
  starting transfers between devices: 13.4 us -> 29.4 us
  waiting for transfers between devices: 96.2 us -> 82.7 us
    all_gather x1 -> x0, waiting for transfers between devices: 61.8 us -> none  [on_device(): everyone = lax.all_gather(exposure, 'cpty', axis=1, tiled=True)]
    ppermute x0 -> x7, waiting for transfers between devices: none -> 47 us  [the longest x4 46.5 us: on_each_block(): next_left = lax.ppermute(from_left, axis, forward) if step < half else None]
    ppermute x0 -> x7, starting transfers between devices: none -> 16.1 us  [the longest x3 9.64 us: on_each_block(): lax.ppermute(from_right, axis, left)]
  transfers between devices with their start and end apart: 4 -> 10, of which waited for: 3 -> 7; matrix products, arithmetic and copies ran while one was open for 8% -> 9% of each run, Pallas kernels for 0% -> 0%
where the time goes in v1:
time: 207 us
  waiting for transfers between devices  82.7 us (40%)
  local copies, waits for them, and re-layouts  56.1 us (27%)
  starting transfers between devices  29.4 us (14%)
  matrix products  15.7 us (8%)
  between operations  14.4 us (7%)
  other arithmetic  8.81 us (4%)
    ppermute x4, waiting for transfers between devices, on_each_block(): next_left = lax.ppermute(from_left, axis, forward) if step < half else None  46.5 us
    gather x1, local copies, waits for them, and re-layouts, on_device(): labels = jnp.where(filled, trade_cpty[chosen], -1)[None, :]  23 us
    reduce_scatter x1, waiting for transfers between devices, on_device(): lax.psum_scatter(on_each_block(exposure, 'cpty', 1, lambda shard, offset:...  21.3 us
    all_to_all x1, waiting for transfers between devices, on_device(): lax.all_to_all(packed, 'cpty', split_axis=1, concat_axis=1, tiled=True)  14.4 us
    dot_general x1, matrix products, on_device(): netted = jnp.dot(arrived, onehot, preferred_element_type=jnp.float32)  13.2 us
    gather x2, local copies, waits for them, and re-layouts, on_device(): jnp.take(described, chosen, axis=1)  12.7 us
    ppermute x3, starting transfers between devices, on_each_block(): lax.ppermute(from_right, axis, left)  9.64 us
    scatter x1, local copies, waits for them, and re-layouts, on_device(): filled = jnp.zeros((groups * slot_size,), jnp.bool_).at[target].set(True)  9.13 us
  transfers between devices with their start and end apart: 10, of which 7 were waited for; matrix products, arithmetic and copies ran while one was open for 9% of the time, Pallas kernels for 0%

profile of v1, /device:TPU:0, one launch (start us, length us, event | category | flops | bytes accessed | tf_op | source)
XLA Modules:
  0.0 207.1 jit_solution(1001644871289091661)
XLA Ops:
  7.2 0.8 add_select_fusion
  8.0 2.3 %reduce-window.6 = s32[8,16,128]{2,1,0:T(8,128)S(1)} reduce-window(s32[8,16,128]{2,1,0:T(8,128)S(1)} %fusion.22, s32[]{:T(128)} %constant.38.clone.1), window={size=1x1x128 pad=0_0x0_0x127_0}, to_apply=%region_0.1 | reduce-window | flops 2080768 | bytes 131076 | tf_op jit(solution)/shard_map/reduce-window
  10.9 0.7 compare_select_fusion.1
  11.6 8.1 %scatter_custom_fusion.1 = s32[4096]{0:T(1024)S(1)} fusion(s32[2048]{0:T(1024)S(1)} %compare_select_fusion.1, s32[2048]{0:T(1024)S(1)} %iota.19, s32[]{:T(128)} %constant.38.clone.1), kind=kCustom, calls=%fused_computation.60 | custom fusion | bytes 16388 | tf_op jit(solution)/shard_map/scatter | solution.py:53
  19.7 23.0 %gather_fusion.1 = s32[4096]{0:T(1024)S(1)} fusion(s32[2048]{0:T(1024)S(1)} %copy-done.1, s32[4096]{0:T(1024)S(1)} %fusion.23), kind=kCustom, calls=%fused_computation.1 | custom fusion | bytes 49152 | tf_op jit(solution)/shard_map/gather | solution.py:56
  42.8 9.1 %scatter_custom_fusion = pred[4096]{0:T(1024)(128)(4,1)S(1)} fusion(s32[2048]{0:T(1024)S(1)} %compare_select_fusion.1, pred[2048]{0:T(1024)(128)(4,1)S(1)} %broadcast.124, pred[]{:T(512)} %constant.30.clone.1), kind=kCustom, calls=%fused_computation.64 | custom fusion | bytes 4097 | tf_op jit(solution)/shard_map/scatter | solution.py:55
  51.9 0.6 broadcast_select_fusion
  52.5 7.3 %all-to-all-start.1 = ((s32[1,8,512]{2,0,1:T(1,128)}), s32[1,8,512]{2,0,1:T(1,128)S(1)}, u32[]{:S(2)}, u32[]{:S(2)}) async-start(s32[1,8,512]{2,0,1:T(1,128)} %bitcast.8), calls=%async_computation.1 | async-start | bytes 32768 | tf_op jit(solution)/shard_map/all_to_all | solution.py:65
  59.9 0.3 stack.50
  60.2 0.3 stack.49
  61.2 0.7 pad_maximum_fusion
  61.9 12.1 %gather_fusion = bf16[4096,67]{1,0:T(8,128)(2,1)S(1)} fusion(bf16[67,2048]{0,1:T(8,128)(2,1)S(1)} %pad_maximum_fusion, s32[4096]{0:T(1024)S(1)} %fusion.23), kind=kCustom, calls=%fused_computation | custom fusion | bytes 1114112 | tf_op jit(solution)/shard_map/jit(_take)/gather | solution.py:61
  74.0 0.6 copy.23
  74.7 0.9 select_select_fusion
  75.6 6.0 %all-to-all-start = ((bf16[67,8,512]{2,0,1:T(8,128)(2,1)}), bf16[67,8,512]{2,0,1:T(8,128)(2,1)S(1)}, u32[]{:S(2)}, u32[]{:S(2)}) async-start(bf16[67,8,512]{2,0,1:T(8,128)(2,1)} %select_select_fusion), calls=%async_computation | async-start | bytes 1179648 | tf_op jit(solution)/shard_map/all_to_all | solution.py:64
  81.6 0.9 iota_compare_fusion.7
  82.5 14.4 %all-to-all-done = bf16[67,8,512]{2,0,1:T(8,128)(2,1)S(1)} async-done(((bf16[67,8,512]{2,0,1:T(8,128)(2,1)}), bf16[67,8,512]{2,0,1:T(8,128)(2,1)S(1)}, u32[]{:S(2)}, u32[]{:S(2)}) %all-to-all-start) | async-done | bytes 548896 | tf_op jit(solution)/shard_map/all_to_all | solution.py:64
  97.1 13.2 %fusion.9 = bf16[1536,128]{1,0:T(8,128)(2,1)S(1)} fusion(bf16[64,4096]{1,0:T(8,128)(2,1)S(1)} %bitcast.118, bf16[64,1536]{1,0:T(8,128)(2,1)S(1)} %copy-done, f32[4096]{0:T(1024)S(1)} %bitcast.123, f32[4096]{0:T(1024)S(1)} %bitcast.124, f32[4096]{0:T(1024)S(1)} %bitcast.122, pred[4096,128]{1,0:T(32,128)(4,1)S(1)} %iota_compare_fusion.7), kind=kOutput, calls=%fused_computation.16 | convolution fusion | flops 2447769600 | bytes 1687552 | tf_op jit(solution)/shard_map/dot_general | solution.py:73
  110.3 1.5 collective-permute-start
  111.8 10.3 %collective-permute-done = bf16[1536,128]{1,0:T(8,128)(2,1)S(1)} collective-permute-done((bf16[1536,128]{1,0:T(8,128)(2,1)S(1)}, bf16[1536,128]{1,0:T(8,128)(2,1)S(1)}, u32[]{:S(2)}, u32[]{:S(2)}) %collective-permute-start) | collective-permute-done | bytes 393248 | tf_op jit(solution)/shard_map/ppermute | solution.py:23
  122.1 4.7 %collective-permute-start.4 = (bf16[1536,128]{1,0:T(8,128)(2,1)S(1)}, bf16[1536,128]{1,0:T(8,128)(2,1)S(1)}, u32[]{:S(2)}, u32[]{:S(2)}) collective-permute-start(bf16[1536,128]{1,0:T(8,128)(2,1)S(1)} %fusion.9), channel_id=1, source_target_pairs={{0,7},{1,0},{2,1},{3,2},{4,3},{5,4},{6,5},{7,6},{8,15},{9,8},{10,9... | collective-permute-start | bytes 1179656 | tf_op jit(solution)/shard_map/ppermute | solution.py:24
  126.9 9.9 %collective-permute-done.1 = bf16[1536,128]{1,0:T(8,128)(2,1)S(1)} collective-permute-done((bf16[1536,128]{1,0:T(8,128)(2,1)S(1)}, bf16[1536,128]{1,0:T(8,128)(2,1)S(1)}, u32[]{:S(2)}, u32[]{:S(2)}) %collective-permute-start.1) | collective-permute-done | bytes 393248 | tf_op jit(solution)/shard_map/ppermute | solution.py:23
  136.8 2.5 %collective-permute-start.2 = (bf16[1536,128]{1,0:T(8,128)(2,1)S(1)}, bf16[1536,128]{1,0:T(8,128)(2,1)S(1)}, u32[]{:S(2)}, u32[]{:S(2)}) collective-permute-start(bf16[1536,128]{1,0:T(8,128)(2,1)S(1)} %collective-permute-done.1), channel_id=1, source_target_pairs={{0,1},{1,2},{2,3},{3,4},{4,5},{5,6},{6,7},{7,0},{8,9},{9,10},{10,1... | collective-permute-start | bytes 1179656 | tf_op jit(solution)/shard_map/ppermute | solution.py:23
  139.3 2.6 %collective-permute-start.5 = (bf16[1536,128]{1,0:T(8,128)(2,1)S(1)}, bf16[1536,128]{1,0:T(8,128)(2,1)S(1)}, u32[]{:S(2)}, u32[]{:S(2)}) collective-permute-start(bf16[1536,128]{1,0:T(8,128)(2,1)S(1)} %collective-permute-done.4), channel_id=1, source_target_pairs={{0,7},{1,0},{2,1},{3,2},{4,3},{5,4},{6,5},{7,6},{8,15},{9,8},{10,9... | collective-permute-start | bytes 1179656 | tf_op jit(solution)/shard_map/ppermute | solution.py:24
  141.9 12.9 %collective-permute-done.2 = bf16[1536,128]{1,0:T(8,128)(2,1)S(1)} collective-permute-done((bf16[1536,128]{1,0:T(8,128)(2,1)S(1)}, bf16[1536,128]{1,0:T(8,128)(2,1)S(1)}, u32[]{:S(2)}, u32[]{:S(2)}) %collective-permute-start.2) | collective-permute-done | bytes 393248 | tf_op jit(solution)/shard_map/ppermute | solution.py:23
  154.9 2.5 %collective-permute-start.3 = (bf16[1536,128]{1,0:T(8,128)(2,1)S(1)}, bf16[1536,128]{1,0:T(8,128)(2,1)S(1)}, u32[]{:S(2)}, u32[]{:S(2)}) collective-permute-start(bf16[1536,128]{1,0:T(8,128)(2,1)S(1)} %collective-permute-done.2), channel_id=1, source_target_pairs={{0,1},{1,2},{2,3},{3,4},{4,5},{5,6},{6,7},{7,0},{8,9},{9,10},{10,1... | collective-permute-start | bytes 1179656 | tf_op jit(solution)/shard_map/ppermute | solution.py:23
  157.4 2.3 %collective-permute-start.6 = (bf16[1536,128]{1,0:T(8,128)(2,1)S(1)}, bf16[1536,128]{1,0:T(8,128)(2,1)S(1)}, u32[]{:S(2)}, u32[]{:S(2)}) collective-permute-start(bf16[1536,128]{1,0:T(8,128)(2,1)S(1)} %collective-permute-done.5), channel_id=1, source_target_pairs={{0,7},{1,0},{2,1},{3,2},{4,3},{5,4},{6,5},{7,6},{8,15},{9,8},{10,9... | collective-permute-start | bytes 1179656 | tf_op jit(solution)/shard_map/ppermute | solution.py:24
  159.7 13.3 %collective-permute-done.3 = bf16[1536,128]{1,0:T(8,128)(2,1)S(1)} collective-permute-done((bf16[1536,128]{1,0:T(8,128)(2,1)S(1)}, bf16[1536,128]{1,0:T(8,128)(2,1)S(1)}, u32[]{:S(2)}, u32[]{:S(2)}) %collective-permute-start.3) | collective-permute-done | bytes 393248 | tf_op jit(solution)/shard_map/ppermute | solution.py:23
  175.1 0.5 collective-permute-done.6
  176.0 1.4 gather_fusion.2
  177.4 21.3 %reduce-scatter.2.cloned.1.call-done = f32[256,128]{1,0:T(8,128)} async-done(((f32[1024,128]{1,0:T(8,128)}), f32[256,128]{1,0:T(8,128)}) %reduce-scatter.2.cloned.1.call-update) | async-done | bytes 131088 | tf_op jit(solution)/shard_map/reduce_scatter | solution.py:77
  198.6 1.6 broadcast_multiply_fusion
  (48 shorter events, 4.0 us)
Async XLA Ops:
  7.2 89.9 %copy-start = (bf16[64,1536]{1,0:T(8,128)(2,1)S(1)}, bf16[64,1536]{1,0:T(8,128)(2,1)}, u32[]{:S(2)}) copy-start(bf16[64,1536]{1,0:T(8,128)(2,1)} %param.6) | copy-start | bytes 589828
  7.2 12.5 %copy-start.1 = (s32[2048]{0:T(1024)S(1)}, s32[2048]{0:T(1024)}, u32[]{:S(2)}) copy-start(s32[2048]{0:T(1024)} %param.11) | copy-start | bytes 24580
  19.7 40.2 %copy-start.4 = (bf16[2048]{0:T(1024)(128)(2,1)S(1)}, bf16[2048]{0:T(1024)(128)(2,1)}, u32[]{:S(2)}) copy-start(bf16[2048]{0:T(1024)(128)(2,1)} %param.10) | copy-start | bytes 12292
  19.7 40.5 %copy-start.5 = (bf16[2048]{0:T(1024)(128)(2,1)S(1)}, bf16[2048]{0:T(1024)(128)(2,1)}, u32[]{:S(2)}) copy-start(bf16[2048]{0:T(1024)(128)(2,1)} %param.9) | copy-start | bytes 12292
  42.7 17.8 %copy-start.6 = (bf16[2048]{0:T(1024)(128)(2,1)S(1)}, bf16[2048]{0:T(1024)(128)(2,1)}, u32[]{:S(2)}) copy-start(bf16[2048]{0:T(1024)(128)(2,1)} %param.8) | copy-start | bytes 12292
  42.7 18.2 %copy-start.3 = (bf16[64,2048]{1,0:T(8,128)(2,1)S(1)}, bf16[64,2048]{1,0:T(8,128)(2,1)}, u32[]{:S(2)}) copy-start(bf16[64,2048]{1,0:T(8,128)(2,1)} %param.7) | copy-start | bytes 786436
  52.5 23.1 %all-to-all-start.1 = ((s32[1,8,512]{2,0,1:T(1,128)}), s32[1,8,512]{2,0,1:T(1,128)S(1)}, u32[]{:S(2)}, u32[]{:S(2)}) async-start(s32[1,8,512]{2,0,1:T(1,128)} %bitcast.8), calls=%async_computation.1 | async-start | bytes 32768 | tf_op jit(solution)/shard_map/all_to_all | solution.py:65
  75.6 21.4 %all-to-all-start = ((bf16[67,8,512]{2,0,1:T(8,128)(2,1)}), bf16[67,8,512]{2,0,1:T(8,128)(2,1)S(1)}, u32[]{:S(2)}, u32[]{:S(2)}) async-start(bf16[67,8,512]{2,0,1:T(8,128)(2,1)} %select_select_fusion), calls=%async_computation | async-start | bytes 1179648 | tf_op jit(solution)/shard_map/all_to_all | solution.py:64
  81.6 117.1 %reduce-scatter.2.cloned.1.call-start = ((), (), s32[]{:S(2)}) async-start(), calls=%async_computation.3 | async-start | bytes 655360 | tf_op jit(solution)/shard_map/reduce_scatter | solution.py:77
  110.3 65.3 %copy-start.2 = (bf16[1536,128]{1,0:T(8,128)(2,1)}, bf16[1536,128]{1,0:T(8,128)(2,1)S(1)}, u32[]{:S(2)}) copy-start(bf16[1536,128]{1,0:T(8,128)(2,1)S(1)} %fusion.9) | copy-start | bytes 1179652
  110.3 11.8 %collective-permute-start = (bf16[1536,128]{1,0:T(8,128)(2,1)S(1)}, bf16[1536,128]{1,0:T(8,128)(2,1)S(1)}, u32[]{:S(2)}, u32[]{:S(2)}) collective-permute-start(bf16[1536,128]{1,0:T(8,128)(2,1)S(1)} %fusion.9), channel_id=1, source_target_pairs={{0,1},{1,2},{2,3},{3,4},{4,5},{5,6},{6,7},{7,0},{8,9},{9,10},{10,1... | collective-permute-start | bytes 1179656 | tf_op jit(solution)/shard_map/ppermute | solution.py:23
  122.1 14.7 %collective-permute-start.1 = (bf16[1536,128]{1,0:T(8,128)(2,1)S(1)}, bf16[1536,128]{1,0:T(8,128)(2,1)S(1)}, u32[]{:S(2)}, u32[]{:S(2)}) collective-permute-start(bf16[1536,128]{1,0:T(8,128)(2,1)S(1)} %collective-permute-done), channel_id=1, source_target_pairs={{0,1},{1,2},{2,3},{3,4},{4,5},{5,6},{6,7},{7,0},{8,9},{9,10},{10,1... | collective-permute-start | bytes 1179656 | tf_op jit(solution)/shard_map/ppermute | solution.py:23
  122.1 17.1 %collective-permute-start.4 = (bf16[1536,128]{1,0:T(8,128)(2,1)S(1)}, bf16[1536,128]{1,0:T(8,128)(2,1)S(1)}, u32[]{:S(2)}, u32[]{:S(2)}) collective-permute-start(bf16[1536,128]{1,0:T(8,128)(2,1)S(1)} %fusion.9), channel_id=1, source_target_pairs={{0,7},{1,0},{2,1},{3,2},{4,3},{5,4},{6,5},{7,6},{8,15},{9,8},{10,9... | collective-permute-start | bytes 1179656 | tf_op jit(solution)/shard_map/ppermute | solution.py:24
  136.8 18.0 %collective-permute-start.2 = (bf16[1536,128]{1,0:T(8,128)(2,1)S(1)}, bf16[1536,128]{1,0:T(8,128)(2,1)S(1)}, u32[]{:S(2)}, u32[]{:S(2)}) collective-permute-start(bf16[1536,128]{1,0:T(8,128)(2,1)S(1)} %collective-permute-done.1), channel_id=1, source_target_pairs={{0,1},{1,2},{2,3},{3,4},{4,5},{5,6},{6,7},{7,0},{8,9},{9,10},{10,1... | collective-permute-start | bytes 1179656 | tf_op jit(solution)/shard_map/ppermute | solution.py:23
  139.3 18.1 %collective-permute-start.5 = (bf16[1536,128]{1,0:T(8,128)(2,1)S(1)}, bf16[1536,128]{1,0:T(8,128)(2,1)S(1)}, u32[]{:S(2)}, u32[]{:S(2)}) collective-permute-start(bf16[1536,128]{1,0:T(8,128)(2,1)S(1)} %collective-permute-done.4), channel_id=1, source_target_pairs={{0,7},{1,0},{2,1},{3,2},{4,3},{5,4},{6,5},{7,6},{8,15},{9,8},{10,9... | collective-permute-start | bytes 1179656 | tf_op jit(solution)/shard_map/ppermute | solution.py:24
  154.9 18.1 %collective-permute-start.3 = (bf16[1536,128]{1,0:T(8,128)(2,1)S(1)}, bf16[1536,128]{1,0:T(8,128)(2,1)S(1)}, u32[]{:S(2)}, u32[]{:S(2)}) collective-permute-start(bf16[1536,128]{1,0:T(8,128)(2,1)S(1)} %collective-permute-done.2), channel_id=1, source_target_pairs={{0,1},{1,2},{2,3},{3,4},{4,5},{5,6},{6,7},{7,0},{8,9},{9,10},{10,1... | collective-permute-start | bytes 1179656 | tf_op jit(solution)/shard_map/ppermute | solution.py:23
  157.4 18.3 %collective-permute-start.6 = (bf16[1536,128]{1,0:T(8,128)(2,1)S(1)}, bf16[1536,128]{1,0:T(8,128)(2,1)S(1)}, u32[]{:S(2)}, u32[]{:S(2)}) collective-permute-start(bf16[1536,128]{1,0:T(8,128)(2,1)S(1)} %collective-permute-done.5), channel_id=1, source_target_pairs={{0,7},{1,0},{2,1},{3,2},{4,3},{5,4},{6,5},{7,6},{8,15},{9,8},{10,9... | collective-permute-start | bytes 1179656 | tf_op jit(solution)/shard_map/ppermute | solution.py:24
Sparse Core Ops, SparseCore 0:
  177.5 21.1 reduce-scatter.1
